TPU v7x, 768 devices: a whole 4x8x12 slice. The times are simulated.
768 devices in a mesh: gx: 64 (over y, x, core), gy: 12 (over z).
Axes of the slice: x: 4, y: 8, z: 12, core: 2. Of those that a mesh axis runs over, the one named last changes fastest.
Arguments:
- displacement: float32 [3, 128, 24, 128], P(None, 'gx', 'gy'), may hold values from -0.3 to 0.3
- velocity: float32 [3, 128, 24, 128], P(None, 'gx', 'gy'), may hold values from -30 to 30
- forces: float32 [3, 128, 24, 128], P(None, 'gx', 'gy'), may hold values from -30 to 30
- heights: int32 [128, 24, 128], P('gx', 'gy'), may hold values from 0 to 127, as said below
- counts: int32 [128, 24], P('gx', 'gy'), may hold values from 64 to 128
- neighbours: int32 [8, 128, 24, 128], P(None, 'gx', 'gy'), may hold values from 0 to 1151, as said below
- plan: int32 [64, 12, 4, 1], P('gx', 'gy'), may hold values from 0 to 11; in each aligned block of 4 rows (0 to 3, 4 to 7, ..., all dimensions but the last counted through in order) at most 2 rows name the same one
Outputs:
- arrived: float32 [64, 12, 12, 2, 7, 128], P('gx', 'gy')
Inputs may be any that keep to these rules, and one draw needn't show every extreme that they name: `heights`: each cell column's 128 entries name every layer from 0 to 127 once. `neighbours`: entry c * 128 + s names slot s of the column at offset (c // 3 - 1, c % 3 - 1) in x and y; a slot never names itself. `plan`: among one device's 2 * 2 cell columns at most 2 name the same new owner.
All inputs are finite; a program needn't handle non-finite values.
Results may differ from a plain program's by a relative error of at most 0.0003.
Values sent between devices are 32-bit elements; how exact they have to be, the bound alone decides.
A program may use at most 32 MiB of HBM per device.

v0:
```python
import jax
import jax.numpy as jnp
from jax import lax
from jax.sharding import PartitionSpec as P

repulse_a = 1830.8
attract_b = 471.18
decay_one = 2.4799
decay_two = 1.7322
beta_t = 1.1e-06
expo_n = 0.78734
coeff_c2 = 100390.0**2
coeff_d2 = 16.217**2
coeff_h = -0.59825
spacing = 2.4
time_step = 0.001
half_step = 0.0005
force_scale = 9648.53 / 28.0855


def shifted(value, axis, steps):
    count = lax.axis_size(axis)
    first, last = (max(0, -steps), min(count, count - steps))
    return lax.ppermute(value, axis, [(source, source + steps) for source in range(first, last)])


def extended(array, sides, width):
    for axis, dim in sides:
        size, length = (lax.axis_size(axis), array.shape[dim])
        up = [(i, (i + 1) % size) for i in range(size - 1)]
        down = [(j, i) for i, j in up]
        last = lax.slice_in_dim(array, length - width, length, axis=dim)
        first = lax.slice_in_dim(array, 0, width, axis=dim)
        before = lax.ppermute(last, axis, up)
        after = lax.ppermute(first, axis, down)
        array = jnp.concatenate([before, array, after], axis=dim)
    return array


def cutoff(radius):
    smooth = 0.5 - 0.5 * jnp.sin(0.5 * jnp.pi * (radius - 2.85) / 0.15)
    return jnp.where(radius < 2.7, 1.0, jnp.where(radius > 3.0, 0.0, smooth))


def cell_energy(center, nearby):
    offsets = nearby[:3] - center[:3][:, :, :, None, :]
    radius = jnp.sqrt(jnp.maximum(jnp.sum(offsets * offsets, axis=0), 1.0))
    weight = cutoff(radius) * nearby[3]
    direction = offsets / radius
    cosine = direction[0][:, :, :, None, :] * direction[0][:, :, None, :, :]
    cosine = cosine + direction[1][:, :, :, None, :] * direction[1][:, :, None, :, :]
    cosine = cosine + direction[2][:, :, :, None, :] * direction[2][:, :, None, :, :]
    spread = (coeff_h - cosine) ** 2
    angular = 1.0 + coeff_c2 * spread / (coeff_d2 * (coeff_d2 + spread))
    others = 1.0 - jnp.eye(nearby.shape[3], dtype=cosine.dtype)[:, :, None]
    bond_sum = jnp.maximum(jnp.sum(angular * weight[:, :, None, :, :] * others, axis=3), 1.0)
    bond_order = (1.0 + jnp.exp(expo_n * jnp.log(beta_t * bond_sum))) ** (-0.5 / expo_n)
    pair_terms = weight * (
        repulse_a * jnp.exp(-decay_one * radius)
        - attract_b * jnp.exp(-decay_two * radius) * bond_order
    )
    return 0.5 * center[3] * jnp.sum(pair_terms, axis=2)


def flat_index(neighbours):
    width_x, width_y = (neighbours.shape[1], neighbours.shape[2])
    return jnp.transpose(neighbours, (1, 2, 0, 3)).reshape(width_x, width_y, -1)


def gather_nearby(points, gather_index):
    width_x, width_y = (gather_index.shape[0], gather_index.shape[1])
    slots = points.shape[3]
    pieces = [
        points[:, 1 + shift_x : 1 + shift_x + width_x, 1 + shift_y : 1 + shift_y + width_y]
        for shift_x in (-1, 0, 1)
        for shift_y in (-1, 0, 1)
    ]
    joined = jnp.concatenate(pieces, axis=3)
    wide_index = jnp.broadcast_to(gather_index[None], (4,) + gather_index.shape)
    picked = jnp.take_along_axis(joined, wide_index, axis=3)
    return picked.reshape(4, width_x, width_y, gather_index.shape[2] // slots, slots)


def tersoff_total(coords, occupied, gather_index):
    points = jnp.concatenate([coords, occupied], axis=0)
    center = points[:, 1:-1, 1:-1]
    return jnp.sum(cell_energy(center, gather_nearby(points, gather_index)))


def return_y(strip, offset):
    return shifted(strip, "gy", offset)


def return_x(strip, offset):
    return shifted(strip, "gx", offset)


def forces_returned(state, gather_index):
    padded = extended(state, (("gx", 1), ("gy", 2)), 1)
    grads = jax.grad(tersoff_total)(padded[:3], padded[3:], gather_index)
    width_y = grads.shape[2] - 2
    from_above = return_y(grads[:, :, 0], -1)
    from_below = return_y(grads[:, :, width_y + 1], 1)
    grads = grads.at[:, :, width_y].add(from_above).at[:, :, 1].add(from_below)[:, :, 1:-1]
    width_x = grads.shape[1] - 2
    from_right = return_x(grads[:, 0], -1)
    from_left = return_x(grads[:, width_x + 1], 1)
    grads = grads.at[:, width_x].add(from_right).at[:, 1].add(from_left)[:, 1:-1]
    return -grads


def pack_columns(rows, plan_rows, groups, capacity):
    target = plan_rows[:, 0]
    chosen = (target[:, None] == jnp.arange(groups, dtype=jnp.int32)[None, :]).astype(jnp.int32)
    earlier = jnp.cumsum(chosen, axis=0) - chosen
    place = target * capacity + jnp.sum(chosen * earlier, axis=1)
    dispatch = (jnp.arange(groups * capacity, dtype=jnp.int32)[:, None] == place[None, :]).astype(
        rows.dtype
    )
    packed = jnp.einsum("rc,acs->ras", dispatch, rows, precision=lax.Precision.HIGHEST)
    return packed.reshape(groups, capacity, rows.shape[0], rows.shape[2])


def per_device(displacement, velocity, forces, heights, counts, neighbours, plan):
    cells_x, cells_y, slots = heights.shape
    first_x = lax.axis_index("gx") * cells_x
    first_y = lax.axis_index("gy") * cells_y
    along_x = ((first_x + jnp.arange(cells_x, dtype=jnp.int32)).astype(jnp.float32) + 0.5) * spacing
    along_y = ((first_y + jnp.arange(cells_y, dtype=jnp.int32)).astype(jnp.float32) + 0.5) * spacing
    along_z = (heights.astype(jnp.float32) + 0.5) * spacing
    lattice = jnp.stack(
        [
            jnp.broadcast_to(along_x[:, None, None], along_z.shape),
            jnp.broadcast_to(along_y[None, :, None], along_z.shape),
            along_z,
        ]
    )
    occupied = (heights < counts[:, :, None]).astype(jnp.float32)
    gather_index = flat_index(neighbours)
    offset, speed, force_now = (displacement, velocity, forces)
    speed = speed + half_step * (force_now * force_scale)
    offset = offset + time_step * speed
    state = jnp.concatenate([lattice + offset, occupied[None]], axis=0)
    force_now = forces_returned(state, gather_index)
    speed = speed + half_step * (force_now * force_scale)
    columns = cells_x * cells_y
    groups = lax.axis_size("gy")
    capacity = max(2, (2 * columns + groups - 1) // groups)
    rows = jnp.concatenate([offset, speed, occupied[None]], axis=0).reshape(7, columns, slots)
    packed = pack_columns(rows, plan[0, 0], groups, capacity)
    arrived = lax.all_to_all(packed, "gy", split_axis=0, concat_axis=0, tiled=True)
    return arrived[None, None]


def solution(mesh):
    in_specs = (
        P(None, "gx", "gy", None),
        P(None, "gx", "gy", None),
        P(None, "gx", "gy", None),
        P("gx", "gy", None),
        P("gx", "gy"),
        P(None, "gx", "gy", None),
        P("gx", "gy", None, None),
    )
    out_specs = P("gx", "gy", None, None, None, None)
    return jax.shard_map(
        per_device, mesh=mesh, in_specs=in_specs, out_specs=out_specs, check_vma=False
    )
```

profile of v0, /device:TPU:32, one launch (start us, length us, event | category | flops | bytes accessed | tf_op | source)
XLA Modules:
  0.0 344.6 jit_solution(11634905783602105024)
XLA Ops:
  0.0 0.7 fusion.35
  0.9 0.7 maximum_add_fusion
  1.6 0.8 fusion.40
  2.4 1.9 collective-permute-start
  4.3 7.0 %collective-permute-start.1 = (f32[4,1,2,128]{3,0,2,1:T(4,128)S(1)}, f32[4,1,2,128]{3,0,2,1:T(4,128)S(1)}, u32[]{:S(2)}, u32[]{:S(2)}) collective-permute-start(f32[4,1,2,128]{3,0,2,1:T(4,128)S(1)} %get-tuple-element.100), channel_id=1, source_target_pairs={{12,0},{24,12},{36,24},{48,36},{60,48},{72,60},{84,72},{96,84},{10... | collective-permute-start | bytes 12296 | tf_op jit(solution)/shard_map/ppermute | solution.py:35
  11.4 0.8 broadcast_select_fusion.2
  12.1 0.7 fusion.36
  13.3 0.4 copy-done.4
  13.7 0.3 and_reduce_fusion
  14.3 4.3 %collective-permute-start.2 = (f32[4,4,1,128]{3,0,2,1:T(4,128)S(1)}, f32[4,4,1,128]{3,0,2,1:T(4,128)S(1)}, u32[]{:S(2)}, u32[]{:S(2)}) collective-permute-start(f32[4,4,1,128]{3,0,2,1:T(4,128)S(1)} %get-tuple-element.98), channel_id=1, source_target_pairs={{0,1},{1,2},{2,3},{3,4},{4,5},{5,6},{6,7},{7,8},{8,9},{9,10},{10,1... | collective-permute-start | bytes 24584 | tf_op jit(solution)/shard_map/ppermute | solution.py:34
  18.6 1.3 collective-permute-start.3
  20.0 4.5 %collective-permute-done.3 = f32[4,4,1,128]{3,0,2,1:T(4,128)S(1)} collective-permute-done((f32[4,4,1,128]{3,0,2,1:T(4,128)S(1)}, f32[4,4,1,128]{3,0,2,1:T(4,128)S(1)}, u32[]{:S(2)}, u32[]{:S(2)}) %collective-permute-start.3) | collective-permute-done | bytes 8224 | tf_op jit(solution)/shard_map/ppermute | solution.py:35
  24.6 174.1 %gather_fusion = f32[16384]{0:T(1024)S(1)} fusion(f32[4,2,2,1152]{3,0,2,1:T(4,128)S(1)} %constant_dynamic-update-slice_fusion, s32[16384]{0:T(1024)S(1)} %bitcast.84), kind=kCustom, calls=%fused_computation | custom fusion | bytes 393216 | tf_op jit(solution)/shard_map/jvp(jit(take_along_axis))/gather | solution.py:80
  199.7 0.3 multiply_reduce_fusion.6
  200.4 97.0 %scatter_custom_fusion = f32[18432]{0:T(1024)S(1)} fusion(s32[16384]{0:T(1024)S(1)} %bitcast.107, f32[16384]{0:T(1024)S(1)} %bitcast.108, f32[]{:T(128)} %constant.179.clone.1), kind=kCustom, calls=%fused_computation.38 | custom fusion | flops 16384 | bytes 73732
  297.6 1.3 collective-permute-start.4
  298.9 4.7 %collective-permute-start.5 = (f32[3,4,128]{2,1,0:T(4,128)S(1)}, f32[3,4,128]{2,1,0:T(4,128)S(1)}, u32[]{:S(2)}, u32[]{:S(2)}) collective-permute-start(f32[3,4,128]{2,1,0:T(4,128)S(1)} %bitcast.112), channel_id=1, source_target_pairs={{0,1},{1,2},{2,3},{3,4},{4,5},{5,6},{6,7},{7,8},{8,9},{9,10},{10,1... | collective-permute-start | bytes 18440 | tf_op jit(solution)/shard_map/ppermute | solution.py:24
  303.6 1.3 collective-permute-done.5
  305.0 3.3 collective-permute-start.6
  308.3 1.9 collective-permute-start.7
  310.3 6.2 %collective-permute-done.7 = f32[3,2,128]{2,1,0:T(2,128)S(1)} collective-permute-done((f32[3,2,128]{2,1,0:T(2,128)S(1)}, f32[3,2,128]{2,1,0:T(2,128)S(1)}, u32[]{:S(2)}, u32[]{:S(2)}) %collective-permute-start.7) | collective-permute-done | bytes 3104 | tf_op jit(solution)/shard_map/ppermute | solution.py:24
  316.7 0.3 fusion.20
  317.1 26.9 %all_to_all.5 = f32[12,2,7,128]{3,1,2,0:T(2,128)S(1)} all-to-all(f32[12,2,7,128]{3,1,2,0:T(2,128)S(1)} %copy.110), channel_id=1, replica_groups=mesh['gx'=64,'gy'=12] {'gy'}, dimensions={0} | all-to-all | bytes 172032 | tf_op jit(solution)/shard_map/all_to_all | solution.py:151
  344.0 0.6 copy.165
  (98 shorter events, 2.6 us)
Async XLA Ops:
  0.0 11.3 %copy-start = (s32[8,2,2,128]{3,2,1,0:T(2,128)S(1)}, s32[8,2,2,128]{3,2,1,0:T(2,128)}, u32[]{:S(2)}) copy-start(s32[8,2,2,128]{3,2,1,0:T(2,128)} %param.20) | copy-start | bytes 49156
  1.6 11.4 %copy-start.5 = (s32[4]{0:T(128)S(1)}, s32[4]{0:T(128)}, u32[]{:S(2)}) copy-start(s32[4]{0:T(128)} %constant.252) | copy-start | bytes 52
  2.4 11.8 %collective-permute-start = (f32[4,1,2,128]{3,0,2,1:T(4,128)S(1)}, f32[4,1,2,128]{3,0,2,1:T(4,128)S(1)}, u32[]{:S(2)}, u32[]{:S(2)}) collective-permute-start(f32[4,1,2,128]{3,0,2,1:T(4,128)S(1)} %get-tuple-element.99), channel_id=1, source_target_pairs={{0,12},{12,24},{24,36},{36,48},{48,60},{60,72},{72,84},{84,96},{96... | collective-permute-start | bytes 12296 | tf_op jit(solution)/shard_map/ppermute | solution.py:34
  4.3 9.9 %collective-permute-start.1 = (f32[4,1,2,128]{3,0,2,1:T(4,128)S(1)}, f32[4,1,2,128]{3,0,2,1:T(4,128)S(1)}, u32[]{:S(2)}, u32[]{:S(2)}) collective-permute-start(f32[4,1,2,128]{3,0,2,1:T(4,128)S(1)} %get-tuple-element.100), channel_id=1, source_target_pairs={{12,0},{24,12},{36,24},{48,36},{60,48},{72,60},{84,72},{96,84},{10... | collective-permute-start | bytes 12296 | tf_op jit(solution)/shard_map/ppermute | solution.py:35
  13.0 0.7 copy-start.4
  13.3 0.8 copy-start.3
  14.3 5.7 %collective-permute-start.2 = (f32[4,4,1,128]{3,0,2,1:T(4,128)S(1)}, f32[4,4,1,128]{3,0,2,1:T(4,128)S(1)}, u32[]{:S(2)}, u32[]{:S(2)}) collective-permute-start(f32[4,4,1,128]{3,0,2,1:T(4,128)S(1)} %get-tuple-element.98), channel_id=1, source_target_pairs={{0,1},{1,2},{2,3},{3,4},{4,5},{5,6},{6,7},{7,8},{8,9},{9,10},{10,1... | collective-permute-start | bytes 24584 | tf_op jit(solution)/shard_map/ppermute | solution.py:34
  18.6 5.9 %collective-permute-start.3 = (f32[4,4,1,128]{3,0,2,1:T(4,128)S(1)}, f32[4,4,1,128]{3,0,2,1:T(4,128)S(1)}, u32[]{:S(2)}, u32[]{:S(2)}) collective-permute-start(f32[4,4,1,128]{3,0,2,1:T(4,128)S(1)} %get-tuple-element.97), channel_id=1, source_target_pairs={{1,0},{2,1},{3,2},{4,3},{5,4},{6,5},{7,6},{8,7},{9,8},{10,9},{11,1... | collective-permute-start | bytes 24584 | tf_op jit(solution)/shard_map/ppermute | solution.py:35
  297.5 19.1 %copy-start.1 = (f32[3,2,2,128]{3,2,1,0:T(2,128)S(1)}, f32[3,2,2,128]{3,2,1,0:T(2,128)}, u32[]{:S(2)}) copy-start(f32[3,2,2,128]{3,2,1,0:T(2,128)} %param.17) | copy-start | bytes 18436
  297.5 19.1 %copy-start.2 = (f32[3,2,2,128]{3,2,1,0:T(2,128)S(1)}, f32[3,2,2,128]{3,2,1,0:T(2,128)}, u32[]{:S(2)}) copy-start(f32[3,2,2,128]{3,2,1,0:T(2,128)} %param.16) | copy-start | bytes 18436
  297.6 6.0 %collective-permute-start.4 = (f32[3,4,128]{2,1,0:T(4,128)S(1)}, f32[3,4,128]{2,1,0:T(4,128)S(1)}, u32[]{:S(2)}, u32[]{:S(2)}) collective-permute-start(f32[3,4,128]{2,1,0:T(4,128)S(1)} %bitcast.113), channel_id=1, source_target_pairs={{1,0},{2,1},{3,2},{4,3},{5,4},{6,5},{7,6},{8,7},{9,8},{10,9},{11,1... | collective-permute-start | bytes 18440 | tf_op jit(solution)/shard_map/ppermute | solution.py:24
  298.9 6.0 %collective-permute-start.5 = (f32[3,4,128]{2,1,0:T(4,128)S(1)}, f32[3,4,128]{2,1,0:T(4,128)S(1)}, u32[]{:S(2)}, u32[]{:S(2)}) collective-permute-start(f32[3,4,128]{2,1,0:T(4,128)S(1)} %bitcast.112), channel_id=1, source_target_pairs={{0,1},{1,2},{2,3},{3,4},{4,5},{5,6},{6,7},{7,8},{8,9},{9,10},{10,1... | collective-permute-start | bytes 18440 | tf_op jit(solution)/shard_map/ppermute | solution.py:24
  305.0 5.3 %collective-permute-start.6 = (f32[3,2,128]{2,1,0:T(2,128)S(1)}, f32[3,2,128]{2,1,0:T(2,128)S(1)}, u32[]{:S(2)}, u32[]{:S(2)}) collective-permute-start(f32[3,2,128]{2,1,0:T(2,128)S(1)} %bitcast.114), channel_id=1, source_target_pairs={{12,0},{24,12},{36,24},{48,36},{60,48},{72,60},{84,72},{96,84},{10... | collective-permute-start | bytes 9224 | tf_op jit(solution)/shard_map/ppermute | solution.py:24
  308.3 8.2 %collective-permute-start.7 = (f32[3,2,128]{2,1,0:T(2,128)S(1)}, f32[3,2,128]{2,1,0:T(2,128)S(1)}, u32[]{:S(2)}, u32[]{:S(2)}) collective-permute-start(f32[3,2,128]{2,1,0:T(2,128)S(1)} %bitcast.115), channel_id=1, source_target_pairs={{0,12},{12,24},{24,36},{36,48},{48,60},{60,72},{72,84},{84,96},{96... | collective-permute-start | bytes 9224 | tf_op jit(solution)/shard_map/ppermute | solution.py:24
where the time goes:
time: 345 us
  local copies, waits for them, and re-layouts  176 us (51%)
  other arithmetic  103 us (30%)
  blocking collectives  26.9 us (8%)
  starting transfers between devices  25.6 us (7%)
  waiting for transfers between devices  12 us (3%)
    gather x2, local copies, waits for them, and re-layouts, gather_nearby(): picked = jnp.take_along_axis(joined, wide_index, axis=3)  174 us
    unnamed x7, other arithmetic  97.7 us
    all_to_all x1, blocking collectives, per_device(): lax.all_to_all(packed, 'gy', split_axis=0, concat_axis=0, tiled=True)  26.9 us
    ppermute x4, starting transfers between devices, shifted(): lax.ppermute(value, axis, [(source, source + steps) for source in range(f...  11.2 us
    ppermute x2, starting transfers between devices, extended(): after = lax.ppermute(first, axis, down)  8.25 us
    ppermute x4, waiting for transfers between devices, shifted(): lax.ppermute(value, axis, [(source, source + steps) for source in range(f...  7.55 us
  transfers between devices with their start and end apart: 8, of which 3 were waited for; matrix products, arithmetic and copies ran while one was open for 1% of the time, Pallas kernels for 0%

commit v1 on v0

v1 whole, which is shorter than its diff:
```python
import functools

import jax
import jax.numpy as jnp
from jax import lax
from jax.experimental import pallas as pl
from jax.experimental.pallas import tpu as pltpu
from jax.sharding import PartitionSpec as P

repulse_a = 1830.8
attract_b = 471.18
decay_one = 2.4799
decay_two = 1.7322
beta_t = 1.1e-06
expo_n = 0.78734
coeff_c2 = 100390.0**2
coeff_d2 = 16.217**2
coeff_h = -0.59825
spacing = 2.4
time_step = 0.001
half_step = 0.0005
force_scale = 9648.53 / 28.0855

FAR = 10000.0
MESH = pl.DeviceIdType.MESH
UNROLL = 4

SIDES = [(dx, dy) for dx in (-1, 0, 1) for dy in (-1, 0, 1) if (dx, dy) != (0, 0)]


def place_of(dx, dy):
    return (dx + 1) * 3 + dy + 1


def near(d):
    return {-1: (0,), 0: (0, 1), 1: (1,)}[d]


LISTS = [(dx, dy, i, j) for dx, dy in SIDES for i in near(dx) for j in near(dy)]


def poly_sin(x):
    y = x * x
    p = -1.0 / 39916800.0
    for c in (1.0 / 362880.0, -1.0 / 5040.0, 1.0 / 120.0, -1.0 / 6.0, 1.0):
        p = p * y + c
    return p * x


def poly_cos(x):
    y = x * x
    p = 1.0 / 479001600.0
    for c in (-1.0 / 3628800.0, 1.0 / 40320.0, -1.0 / 720.0, 1.0 / 24.0, -0.5, 1.0):
        p = p * y + c
    return p


def turn(x, by):
    return pltpu.roll(x, (8 - by) % 8, 0)


def above(value, limit):
    return jnp.where(value > limit, 1.0, jnp.where(value == limit, 0.5, 0.0))


def column_terms(center, near_by):
    occupied = jnp.where(center[2] < 0.5 * FAR, 0.5, 0.0)
    d = [q - p for q, p in zip(near_by, center)]
    square = d[0] * d[0] + d[1] * d[1] + d[2] * d[2]
    clipped = jnp.maximum(square, 1.0)
    inverse = lax.rsqrt(clipped)
    radius = clipped * inverse
    n = [c * inverse for c in d]
    angle = (jnp.clip(radius, 2.7, 3.0) - 2.85) * (0.5 * jnp.pi / 0.15)
    inner, outer = radius < 2.7, radius > 3.0
    w = jnp.where(inner, 1.0, jnp.where(outer, 0.0, 0.5 - 0.5 * poly_sin(angle)))
    slope = jnp.where(inner | outer, 0.0, poly_cos(angle) * (-0.25 * jnp.pi / 0.15))
    turned_n, turned_w, angular, dangular = {}, {}, {}, {}
    zeta = jnp.zeros_like(w)
    for by in (1, 2, 3, 4):
        tn = [turn(c, by) for c in n]
        tw = turn(w, by)
        cosine = n[0] * tn[0] + n[1] * tn[1] + n[2] * tn[2]
        apart = coeff_h - cosine
        spread = apart * apart
        part = 1.0 / (coeff_d2 + spread)
        g = 1.0 + (coeff_c2 / coeff_d2) * spread * part
        zeta = zeta + tw * g
        if by != 4:
            zeta = zeta + turn(w * g, 8 - by)
        turned_n[by], turned_w[by], angular[by] = tn, tw, g
        dangular[by] = (-2.0 * coeff_c2) * apart * (part * part)
    bond = jnp.maximum(zeta, 1.0)
    grown = jnp.exp(expo_n * jnp.log(beta_t * bond))
    order = jnp.exp((-0.5 / expo_n) * jnp.log(1.0 + grown))
    pull = attract_b * jnp.exp(-decay_two * radius)
    push = repulse_a * jnp.exp(-decay_one * radius)
    dzeta = (
        occupied * w * pull * (0.5 * order) * grown / ((1.0 + grown) * bond) * above(zeta, 1.0)
    )
    dw = occupied * (push - pull * order)
    dn = [jnp.zeros_like(w)] * 3
    for by in (1, 2, 3, 4):
        tz = turn(dzeta, by)
        pair = (dzeta * turned_w[by] + tz * w) * dangular[by]
        dw = dw + tz * angular[by]
        for axis in range(3):
            dn[axis] = dn[axis] + pair * turned_n[by][axis]
        if by != 4:
            dw = dw + turn(dzeta * angular[by], 8 - by)
            for axis in range(3):
                dn[axis] = dn[axis] + turn(pair * n[axis], 8 - by)
    dr = occupied * w * (decay_two * pull * order - decay_one * push) + dw * slope
    along = n[0] * dn[0] + n[1] * dn[1] + n[2] * dn[2]
    radial = (dr - along * inverse) * above(square, 1.0)
    return [dn[axis] * inverse + radial * n[axis] for axis in range(3)]


def kernel(
    gx, gy,
    displacement, velocity, forces, heights, counts, neighbours, plan,
    out,
    disp_v, vel_v, for_v, hei_v, nei_v, count_s, plan_s,
    pos, grid_pos, lists, split, terms, speed_v, up, vp, send_u, send_v, got_u, got_v,
    local_sem, pos_send, pos_recv, list_send, list_recv, u_send, u_recv, v_send, v_recv,
):
    a, b = lax.axis_index("gx"), lax.axis_index("gy")

    def at(da, db):
        return lax.rem(a + da + gx, gx), lax.rem(b + db + gy, gy)

    barrier = pltpu.get_barrier_semaphore()
    partners = [at(0, db) for db in range(1, gy)]
    partners += [at(da, db) for da in (-1, 1) for db in (-1, 0, 1)]
    for partner in partners:
        pl.semaphore_signal(barrier, inc=1, device_id=partner, device_id_type=MESH)

    loads = [
        pltpu.make_async_copy(source, target, local_sem.at[number])
        for number, (source, target) in enumerate(
            [
                (displacement, disp_v), (velocity, vel_v), (forces, for_v), (heights, hei_v),
                (neighbours, nei_v), (counts, count_s), (plan, plan_s),
            ]
        )
    ]
    for load in loads:
        load.start()
    for load in loads:
        load.wait()

    for i in range(2):
        high = hei_v[i]
        row = lax.broadcasted_iota(jnp.int32, (2, 128), 0)
        live = high < jnp.where(row == 0, count_s[i, 0], count_s[i, 1])
        occupied = live.astype(jnp.float32)
        for axis in range(3):
            speed = vel_v[axis, i] + half_step * (for_v[axis, i] * force_scale)
            offset = disp_v[axis, i] + time_step * speed
            if axis == 0:
                site = ((2 * a + i).astype(jnp.float32) + 0.5) * spacing
            elif axis == 1:
                site = ((2 * b + row).astype(jnp.float32) + 0.5) * spacing
            else:
                site = (high.astype(jnp.float32) + 0.5) * spacing
            where = site + offset
            if axis == 2:
                where = jnp.where(live, where, where + FAR)
            pos[4, axis * 4 + 2 * i : axis * 4 + 2 * i + 2, :] = where
            for j in range(2):
                speed_v[2 * i + j, axis : axis + 1, :] = speed[j : j + 1]
                up[2 * i + j, axis : axis + 1, :] = offset[j : j + 1]
                up[2 * i + j, axis + 4 : axis + 5, :] = offset[j : j + 1]
        for j in range(2):
            up[2 * i + j, 3:4, :] = occupied[j : j + 1]
            up[2 * i + j, 7:8, :] = occupied[j : j + 1]
            lists[5 + 4 * i + j] = nei_v[:, i, j, :]

    owners = [plan_s[0, 0, c, 0] for c in range(4)]
    place = []
    for c in range(4):
        earlier = jnp.int32(0)
        for e in range(c):
            earlier = earlier + jnp.where(owners[e] == owners[c], 1, 0)
        place.append(owners[c] * 2 + earlier)

    def dealt(rows, half, columns):
        second = (lax.broadcasted_iota(jnp.int32, (rows, 128), 0) >= half).astype(jnp.int32)
        slot = [place[c] - second for c in range(4)]

        def of(owner):
            total = jnp.zeros((rows, 128), jnp.float32)
            for c in range(4):
                total = jnp.where(slot[c] == 2 * owner, columns[c], total)
            return total

        return of

    of_u = dealt(8, 4, [up[c] for c in range(4)])
    for d in range(1, gy):
        send_u[d] = of_u(lax.rem(b + d, gy))
    got_u[b] = of_u(b)

    pl.semaphore_wait(barrier, len(partners))

    copies = []
    for number, (dx, dy) in enumerate(SIDES):
        copies.append(
            pltpu.make_async_remote_copy(
                src_ref=pos.at[4],
                dst_ref=pos.at[place_of(-dx, -dy)],
                send_sem=pos_send.at[number],
                recv_sem=pos_recv.at[number],
                device_id=at(dx, dy),
                device_id_type=MESH,
            )
        )
    for number, (dx, dy, i, j) in enumerate(LISTS):
        x, y = 1 + i - 2 * dx, 1 + j - 2 * dy
        copies.append(
            pltpu.make_async_remote_copy(
                src_ref=lists.at[5 + 4 * i + j],
                dst_ref=lists.at[4 * x + y],
                send_sem=list_send.at[number],
                recv_sem=list_recv.at[number],
                device_id=at(dx, dy),
                device_id_type=MESH,
            )
        )
    for copy in copies:
        copy.start()
    u_copies = []
    for d in range(1, gy):
        u_copies.append(
            pltpu.make_async_remote_copy(
                src_ref=send_u.at[d],
                dst_ref=got_u.at[b],
                send_sem=u_send.at[d],
                recv_sem=u_recv.at[d],
                device_id=at(0, d),
                device_id_type=MESH,
            )
        )
    for copy in u_copies:
        copy.start()
    for copy in copies:
        copy.wait_recv()

    for dx in (-1, 0, 1):
        for dy in (-1, 0, 1):
            gone = ((a + dx) < 0) | ((a + dx) >= gx) | ((b + dy) < 0) | ((b + dy) >= gy)
            lift = jnp.where(gone, FAR, 0.0)
            for axis in range(3):
                for i in range(2):
                    first = axis * 36 + (2 * dx + 2 + i) * 6 + 2 * dy + 2
                    rows = pos[place_of(dx, dy), axis * 4 + 2 * i : axis * 4 + 2 * i + 2, :]
                    grid_pos[first : first + 2, :] = rows + lift if axis == 2 else rows

    rows16 = [
        (lax.broadcasted_iota(jnp.int32, (16, 128), 0) + 16 * k).astype(jnp.float32).astype(jnp.bfloat16)
        for k in range(8)
    ]
    one, none = jnp.ones((16, 128), jnp.bfloat16), jnp.zeros((16, 128), jnp.bfloat16)

    def column(k, part, total):
        x, y = 1 + k // 4, 1 + k % 4
        base = (x - 1) * 6 + y - 1
        entries = lists[k]
        slot, offset = entries & 127, entries >> 7
        near_by = [None] * 3
        for c in range(9):
            here = base + (c // 3) * 6 + c % 3
            for axis in range(3):
                source = jnp.broadcast_to(grid_pos[pl.ds(axis * 36 + here, 1), :], (8, 128))
                taken = jnp.take_along_axis(source, slot, axis=1)
                near_by[axis] = taken if c == 0 else jnp.where(offset == c, taken, near_by[axis])
        center = [
            jnp.broadcast_to(grid_pos[pl.ds(axis * 36 + base + 7, 1), :], (8, 128)) for axis in range(3)
        ]
        grads = column_terms(center, near_by)
        for axis in range(3):
            terms[k, axis] = grads[axis]
        highs = [g.astype(jnp.bfloat16).astype(jnp.float32) for g in grads]
        lows = [g - h for g, h in zip(grads, highs)]
        for t in range(4):
            cx, cy = 3 + t // 2 - x, 3 + t % 2 - y
            inside = (cx >= 0) & (cx <= 2) & (cy >= 0) & (cy <= 2)
            hit = offset == jnp.where(inside, 3 * cx + cy, -1)
            for axis in range(3):
                row = part * 192 + (t * 3 + axis) * 8
                split[pl.ds(row, 8), :] = jnp.where(hit, highs[axis], 0.0)
                split[pl.ds(row + 96, 8), :] = jnp.where(hit, lows[axis], 0.0)
        slot_f = slot.astype(jnp.float32)
        for m in range(0, 8, 2):
            left, right = [], []
            for e in (m, m + 1):
                left.append(split[pl.ds(part * 192 + e, 24, stride=8), :].astype(jnp.bfloat16))
                wanted = jnp.broadcast_to(slot_f[e : e + 1], (16, 128)).astype(jnp.bfloat16)
                right.append(
                    jnp.concatenate([jnp.where(r == wanted, one, none) for r in rows16], axis=0)
                )
            total = total + lax.dot_general(
                jnp.concatenate(left, axis=1),
                jnp.concatenate(right, axis=1),
                (((1,), (1,)), ((), ())),
                preferred_element_type=jnp.float32,
            )
        return total

    def some_columns(step, total):
        for part in range(UNROLL):
            total = column(step * UNROLL + part, part, total)
        return total

    total = lax.fori_loop(0, 16 // UNROLL, some_columns, jnp.zeros((24, 128), jnp.float32))
    on_neighbours = total[0:12] + total[12:24]

    for t in range(4):
        own = 5 + 4 * (t // 2) + t % 2
        for axis in range(3):
            force = jnp.sum(terms[own, axis], axis=0, keepdims=True)
            force = force - on_neighbours[t * 3 + axis : t * 3 + axis + 1]
            speed = speed_v[t, axis : axis + 1, :] + half_step * (force * force_scale)
            vp[t, axis : axis + 1, :] = speed
            vp[t, axis + 3 : axis + 4, :] = speed
    of_v = dealt(6, 3, [vp[c] for c in range(4)])
    v_copies = []
    for d in range(1, gy):
        send_v[d] = of_v(lax.rem(b + d, gy))
        v_copies.append(
            pltpu.make_async_remote_copy(
                src_ref=send_v.at[d],
                dst_ref=got_v.at[b],
                send_sem=v_send.at[d],
                recv_sem=v_recv.at[d],
                device_id=at(0, d),
                device_id_type=MESH,
            )
        )
    for copy in v_copies:
        copy.start()
    got_v[b] = of_v(b)
    for copy in u_copies:
        copy.wait_recv()
    for o in range(gy):
        for s in range(2):
            out[0, 0, o, s, 0:3, :] = got_u[o, 4 * s : 4 * s + 3, :]
            out[0, 0, o, s, 6:7, :] = got_u[o, 4 * s + 3 : 4 * s + 4, :]
    for copy in v_copies:
        copy.wait_recv()
    for o in range(gy):
        for s in range(2):
            out[0, 0, o, s, 3:6, :] = got_v[o, 3 * s : 3 * s + 3, :]
    for copy in copies + u_copies + v_copies:
        copy.wait_send()


def per_device(gx, gy, displacement, velocity, forces, heights, counts, neighbours, plan):
    dma = pltpu.SemaphoreType.DMA
    f32 = jnp.float32
    anywhere = pl.BlockSpec(memory_space=pl.ANY)
    return pl.pallas_call(
        functools.partial(kernel, gx, gy),
        out_shape=jax.ShapeDtypeStruct((1, 1, gy, 2, 7, 128), f32),
        in_specs=[anywhere] * 7,
        out_specs=pl.BlockSpec(memory_space=pltpu.VMEM),
        scratch_shapes=[
            pltpu.VMEM((3, 2, 2, 128), f32),
            pltpu.VMEM((3, 2, 2, 128), f32),
            pltpu.VMEM((3, 2, 2, 128), f32),
            pltpu.VMEM((2, 2, 128), jnp.int32),
            pltpu.VMEM((8, 2, 2, 128), jnp.int32),
            pltpu.SMEM((2, 2), jnp.int32),
            pltpu.SMEM((1, 1, 4, 1), jnp.int32),
            pltpu.VMEM((9, 16, 128), f32),
            pltpu.VMEM((112, 128), f32),
            pltpu.VMEM((16, 8, 128), jnp.int32),
            pltpu.VMEM((UNROLL * 192, 128), f32),
            pltpu.VMEM((16, 3, 8, 128), f32),
            pltpu.VMEM((4, 8, 128), f32),
            pltpu.VMEM((4, 8, 128), f32),
            pltpu.VMEM((4, 6, 128), f32),
            pltpu.VMEM((gy, 8, 128), f32),
            pltpu.VMEM((gy, 6, 128), f32),
            pltpu.VMEM((gy, 8, 128), f32),
            pltpu.VMEM((gy, 6, 128), f32),
            dma((7,)),
            dma((len(SIDES),)),
            dma((len(SIDES),)),
            dma((len(LISTS),)),
            dma((len(LISTS),)),
            dma((gy,)),
            dma((gy,)),
            dma((gy,)),
            dma((gy,)),
        ],
        compiler_params=pltpu.CompilerParams(collective_id=0, has_side_effects=True),
        name="verlet_recut",
    )(displacement, velocity, forces, heights, counts, neighbours, plan)


def solution(mesh):
    in_specs = (
        P(None, "gx", "gy", None),
        P(None, "gx", "gy", None),
        P(None, "gx", "gy", None),
        P("gx", "gy", None),
        P("gx", "gy"),
        P(None, "gx", "gy", None),
        P("gx", "gy", None, None),
    )
    out_specs = P("gx", "gy", None, None, None, None)
    gx, gy = mesh.shape["gx"], mesh.shape["gy"]
    return jax.shard_map(
        functools.partial(per_device, gx, gy),
        mesh=mesh, in_specs=in_specs, out_specs=out_specs, check_vma=False,
    )
```

time: 345 us -> 34.3 us (0.10)
  the two profiles are of different devices: /device:TPU:32 before, /device:TPU:40 now
where the time goes in v1:
time: 34.3 us; the launch traced here: 34.1 us
  Pallas kernels  31.2 us (91%)
  local copies, waits for them, and re-layouts  2.89 us (8%)
    pallas_call x1, Pallas kernels, per_device(): pl.pallas_call(functools.partial(kernel, gx, gy), out_shape=jax.ShapeDtyp...  31.2 us
    pallas_call x1, local copies, waits for them, and re-layouts, per_device(): pl.pallas_call(functools.partial(kernel, gx, gy), out_shape=jax.ShapeDtyp...  1.57 us
    unnamed x1, local copies, waits for them, and re-layouts  1.31 us

profile of v1, /device:TPU:40, one launch (start us, length us, event | category | flops | bytes accessed | tf_op | source)
XLA Modules:
  0.0 34.1 jit_solution(13052416596942306900)
XLA Ops:
  0.0 1.3 %copy.8.plan = s32[1,1,4,1]{3,2,1,0:T(4,128)} copy(s32[1,1,4,1]{2,3,1,0:T(1,128)} %param.13) | data formatting | bytes 32 | tf_op args[6]
  1.3 31.2 %verlet_recut.1 = f32[1,1,12,2,7,128]{5,4,3,2,1,0:T(8,128)} custom-call(f32[3,2,2,128]{3,2,1,0:T(2,128)} %displacement.1, f32[3,2,2,128]{3,2,1,0:T(2,128)} %velocity.1, f32[3,2,2,128]{3,2,1,0:T(2,128)} %forces.1, s32[2,2,128]{2,1,0:T(2,128)} %heights.1, s32[2,2]{1,0:T(2,128)} %counts.1, s32[8,2,2,128]{3,2,1,0:T(2,128)} %neighbours.1, s32[1,1,4,1]{3,2,1,0:T(4,128)} %copy.8.plan), custom_call_target="tpu_custom_call" | custom-call | tf_op jit(solution)/shard_map/verlet_recut/pallas_call | solution.py:362
  32.5 1.6 %copy.9 = f32[1,1,12,2,7,128]{5,3,4,2,1,0:T(2,128)} copy(f32[1,1,12,2,7,128]{5,4,3,2,1,0:T(8,128)} %verlet_recut.1) | data formatting | bytes 172032 | tf_op jit(solution)/shard_map/verlet_recut/pallas_call | solution.py:362

commit v2 on v1

--- a/solution.py
+++ b/solution.py
@@ -24,6 +24,8 @@
 FAR = 10000.0
 MESH = pl.DeviceIdType.MESH
 UNROLL = 4
+REACH = 4
+VMEM_LIMIT = 8 * 1024 * 1024
 
 SIDES = [(dx, dy) for dx in (-1, 0, 1) for dy in (-1, 0, 1) if (dx, dy) != (0, 0)]
 
@@ -122,7 +124,7 @@
     out,
     disp_v, vel_v, for_v, hei_v, nei_v, count_s, plan_s,
     pos, grid_pos, lists, split, terms, speed_v, up, vp, send_u, send_v, got_u, got_v,
-    local_sem, pos_send, pos_recv, list_send, list_recv, u_send, u_recv, v_send, v_recv,
+    local_sem, pos_send, pos_recv, list_send, list_recv, u_send, u_recv, v_send, v_recv, ring,
 ):
     a, b = lax.axis_index("gx"), lax.axis_index("gy")
 
@@ -130,7 +132,8 @@
         return lax.rem(a + da + gx, gx), lax.rem(b + db + gy, gy)
 
     barrier = pltpu.get_barrier_semaphore()
-    partners = [at(0, db) for db in range(1, gy)]
+    greeted = [d for d in range(1, gy) if min(d, gy - d) <= REACH]
+    partners = [at(0, d) for d in greeted]
     partners += [at(da, db) for da in (-1, 1) for db in (-1, 0, 1)]
     for partner in partners:
         pl.semaphore_signal(barrier, inc=1, device_id=partner, device_id_type=MESH)
@@ -166,40 +169,13 @@
             where = site + offset
             if axis == 2:
                 where = jnp.where(live, where, where + FAR)
-            pos[4, axis * 4 + 2 * i : axis * 4 + 2 * i + 2, :] = where
+            pos[4, axis, 2 * i : 2 * i + 2, :] = where
             for j in range(2):
                 speed_v[2 * i + j, axis : axis + 1, :] = speed[j : j + 1]
-                up[2 * i + j, axis : axis + 1, :] = offset[j : j + 1]
-                up[2 * i + j, axis + 4 : axis + 5, :] = offset[j : j + 1]
+                up[2 * i + j, 2 * axis : 2 * axis + 2, :] = jnp.broadcast_to(offset[j : j + 1], (2, 128))
         for j in range(2):
-            up[2 * i + j, 3:4, :] = occupied[j : j + 1]
-            up[2 * i + j, 7:8, :] = occupied[j : j + 1]
+            up[2 * i + j, 6:8, :] = jnp.broadcast_to(occupied[j : j + 1], (2, 128))
             lists[5 + 4 * i + j] = nei_v[:, i, j, :]
-
-    owners = [plan_s[0, 0, c, 0] for c in range(4)]
-    place = []
-    for c in range(4):
-        earlier = jnp.int32(0)
-        for e in range(c):
-            earlier = earlier + jnp.where(owners[e] == owners[c], 1, 0)
-        place.append(owners[c] * 2 + earlier)
-
-    def dealt(rows, half, columns):
-        second = (lax.broadcasted_iota(jnp.int32, (rows, 128), 0) >= half).astype(jnp.int32)
-        slot = [place[c] - second for c in range(4)]
-
-        def of(owner):
-            total = jnp.zeros((rows, 128), jnp.float32)
-            for c in range(4):
-                total = jnp.where(slot[c] == 2 * owner, columns[c], total)
-            return total
-
-        return of
-
-    of_u = dealt(8, 4, [up[c] for c in range(4)])
-    for d in range(1, gy):
-        send_u[d] = of_u(lax.rem(b + d, gy))
-    got_u[b] = of_u(b)
 
     pl.semaphore_wait(barrier, len(partners))
 
@@ -229,22 +205,48 @@
         )
     for copy in copies:
         copy.start()
-    u_copies = []
+    owners = [plan_s[0, 0, 0, c] for c in range(4)]
+    place = []
+    for c in range(4):
+        earlier = jnp.int32(0)
+        for e in range(c):
+            earlier = earlier + jnp.where(owners[e] == owners[c], 1, 0)
+        place.append(owners[c] * 2 + earlier)
+
+    def dealt(rows, columns):
+        second = lax.broadcasted_iota(jnp.int32, (rows, 128), 0) & 1
+        slot = [place[c] - second for c in range(4)]
+
+        def of(owner):
+            total = jnp.zeros((rows, 128), jnp.float32)
+            for c in range(4):
+                total = jnp.where(slot[c] == 2 * owner, columns[c], total)
+            return total
+
+        return of
+
+    of_u = dealt(8, [up[c] for c in range(4)])
     for d in range(1, gy):
-        u_copies.append(
-            pltpu.make_async_remote_copy(
-                src_ref=send_u.at[d],
-                dst_ref=got_u.at[b],
-                send_sem=u_send.at[d],
-                recv_sem=u_recv.at[d],
-                device_id=at(0, d),
-                device_id_type=MESH,
-            )
+        send_u[d] = of_u(lax.rem(b + d, gy))
+    got_u[b] = of_u(b)
+
+    u_copies = {}
+    for d in range(1, gy):
+        u_copies[d] = pltpu.make_async_remote_copy(
+            src_ref=send_u.at[d],
+            dst_ref=got_u.at[b],
+            send_sem=u_send.at[d],
+            recv_sem=u_recv.at[d],
+            device_id=at(0, d),
+            device_id_type=MESH,
         )
-    for copy in u_copies:
-        copy.start()
     for copy in copies:
         copy.wait_recv()
+    known = [d for d in range(1, gy) if min(d, gy - d) <= REACH + 1]
+    for d in known:
+        u_copies[d].start()
+    for d in (1, gy - 1):
+        pl.semaphore_signal(ring, inc=1, device_id=at(0, d), device_id_type=MESH)
 
     for dx in (-1, 0, 1):
         for dy in (-1, 0, 1):
@@ -253,7 +255,7 @@
             for axis in range(3):
                 for i in range(2):
                     first = axis * 36 + (2 * dx + 2 + i) * 6 + 2 * dy + 2
-                    rows = pos[place_of(dx, dy), axis * 4 + 2 * i : axis * 4 + 2 * i + 2, :]
+                    rows = pos[place_of(dx, dy), axis, 2 * i : 2 * i + 2, :]
                     grid_pos[first : first + 2, :] = rows + lift if axis == 2 else rows
 
     rows16 = [
@@ -313,6 +315,10 @@
         return total
 
     total = lax.fori_loop(0, 16 // UNROLL, some_columns, jnp.zeros((24, 128), jnp.float32))
+    pl.semaphore_wait(ring, 2)
+    for d in range(1, gy):
+        if d not in known:
+            u_copies[d].start()
     on_neighbours = total[0:12] + total[12:24]
 
     for t in range(4):
@@ -321,47 +327,45 @@
             force = jnp.sum(terms[own, axis], axis=0, keepdims=True)
             force = force - on_neighbours[t * 3 + axis : t * 3 + axis + 1]
             speed = speed_v[t, axis : axis + 1, :] + half_step * (force * force_scale)
-            vp[t, axis : axis + 1, :] = speed
-            vp[t, axis + 3 : axis + 4, :] = speed
-    of_v = dealt(6, 3, [vp[c] for c in range(4)])
+            vp[t, 2 * axis : 2 * axis + 2, :] = jnp.broadcast_to(speed, (2, 128))
+    of_v = dealt(6, [vp[c] for c in range(4)])
     v_copies = []
-    for d in range(1, gy):
+    for d in sorted(range(1, gy), key=lambda d: -min(d, gy - d)):
         send_v[d] = of_v(lax.rem(b + d, gy))
-        v_copies.append(
-            pltpu.make_async_remote_copy(
-                src_ref=send_v.at[d],
-                dst_ref=got_v.at[b],
-                send_sem=v_send.at[d],
-                recv_sem=v_recv.at[d],
-                device_id=at(0, d),
-                device_id_type=MESH,
-            )
+        copy = pltpu.make_async_remote_copy(
+            src_ref=send_v.at[d],
+            dst_ref=got_v.at[b],
+            send_sem=v_send.at[d],
+            recv_sem=v_recv.at[d],
+            device_id=at(0, d),
+            device_id_type=MESH,
         )
-    for copy in v_copies:
         copy.start()
+        v_copies.append(copy)
     got_v[b] = of_v(b)
-    for copy in u_copies:
+    for copy in u_copies.values():
         copy.wait_recv()
     for o in range(gy):
-        for s in range(2):
-            out[0, 0, o, s, 0:3, :] = got_u[o, 4 * s : 4 * s + 3, :]
-            out[0, 0, o, s, 6:7, :] = got_u[o, 4 * s + 3 : 4 * s + 4, :]
+        for r in range(4):
+            out[0, 0, o, (0, 1, 2, 6)[r], :, :] = got_u[o, 2 * r : 2 * r + 2, :]
     for copy in v_copies:
         copy.wait_recv()
     for o in range(gy):
-        for s in range(2):
-            out[0, 0, o, s, 3:6, :] = got_v[o, 3 * s : 3 * s + 3, :]
-    for copy in copies + u_copies + v_copies:
+        for r in range(3):
+            out[0, 0, o, r + 3, :, :] = got_v[o, 2 * r : 2 * r + 2, :]
+    for copy in copies + list(u_copies.values()) + v_copies:
         copy.wait_send()
 
 
 def per_device(gx, gy, displacement, velocity, forces, heights, counts, neighbours, plan):
     dma = pltpu.SemaphoreType.DMA
     f32 = jnp.float32
-    anywhere = pl.BlockSpec(memory_space=pl.ANY)
-    return pl.pallas_call(
+    anywhere = pl.BlockSpec(memory_space=pltpu.HBM)
+    inputs = [displacement, velocity, forces, heights, counts, neighbours, jnp.swapaxes(plan, 2, 3)]
+    inputs = [pltpu.with_memory_space_constraint(value, pltpu.HBM) for value in inputs]
+    arrived = pl.pallas_call(
         functools.partial(kernel, gx, gy),
-        out_shape=jax.ShapeDtypeStruct((1, 1, gy, 2, 7, 128), f32),
+        out_shape=jax.ShapeDtypeStruct((1, 1, gy, 7, 2, 128), f32),
         in_specs=[anywhere] * 7,
         out_specs=pl.BlockSpec(memory_space=pltpu.VMEM),
         scratch_shapes=[
@@ -371,8 +375,8 @@
             pltpu.VMEM((2, 2, 128), jnp.int32),
             pltpu.VMEM((8, 2, 2, 128), jnp.int32),
             pltpu.SMEM((2, 2), jnp.int32),
-            pltpu.SMEM((1, 1, 4, 1), jnp.int32),
-            pltpu.VMEM((9, 16, 128), f32),
+            pltpu.SMEM((1, 1, 1, 4), jnp.int32),
+            pltpu.VMEM((9, 3, 4, 128), f32),
             pltpu.VMEM((112, 128), f32),
             pltpu.VMEM((16, 8, 128), jnp.int32),
             pltpu.VMEM((UNROLL * 192, 128), f32),
@@ -393,10 +397,14 @@
             dma((gy,)),
             dma((gy,)),
             dma((gy,)),
+            pltpu.SemaphoreType.REGULAR,
         ],
-        compiler_params=pltpu.CompilerParams(collective_id=0, has_side_effects=True),
+        compiler_params=pltpu.CompilerParams(
+            collective_id=0, has_side_effects=True, vmem_limit_bytes=VMEM_LIMIT
+        ),
         name="verlet_recut",
-    )(displacement, velocity, forces, heights, counts, neighbours, plan)
+    )(*inputs)
+    return jnp.swapaxes(arrived, 3, 4)
 
 
 def solution(mesh):

time: 34.3 us -> 31.2 us (0.910)
  the two profiles are of different devices: /device:TPU:40 before, /device:TPU:1 now
where the time goes in v2:
time: 31.2 us; the launch traced here: 31 us
  Pallas kernels  30.4 us (97%)
  local copies, waits for them, and re-layouts  0.64 us (2%)
    pallas_call x1, Pallas kernels, per_device(): pl.pallas_call(functools.partial(kernel, gx, gy), out_shape=jax.ShapeDtyp...  30.4 us
    unnamed x1, local copies, waits for them, and re-layouts  0.64 us

profile of v2, /device:TPU:1, one launch (start us, length us, event | category | flops | bytes accessed | tf_op | source)
XLA Modules:
  0.0 31.0 jit_solution(12603054549121756508)
XLA Ops:
  0.0 30.4 %verlet_recut.1 = f32[1,1,12,7,2,128]{5,4,3,2,1,0:T(2,128)S(1)} custom-call(f32[3,2,2,128]{3,2,1,0:T(2,128)} %displacement.1, f32[3,2,2,128]{3,2,1,0:T(2,128)} %velocity.1, f32[3,2,2,128]{3,2,1,0:T(2,128)} %forces.1, s32[2,2,128]{2,1,0:T(2,128)} %heights.1, s32[2,2]{1,0:T(2,128)} %counts.1, s32[8,2,2,128]{3,2,1,0:T(2,128)} %neighbours.1, s32[1,1,1,4]{3,2,1,0:T(1,128)} %bitcast.3), custom_call_target="tpu_custom_call" | custom-call | tf_op jit(solution)/shard_map/verlet_recut/pallas_call | solution.py:366
  30.4 0.6 %copy.9 = f32[1,1,12,2,7,128]{5,3,4,2,1,0:T(2,128)} copy(f32[1,1,12,2,7,128]{5,3,4,2,1,0:T(2,128)S(1)} %bitcast.2) | data formatting | bytes 172032

commit v3 on v2

--- a/solution.py
+++ b/solution.py
@@ -24,10 +24,12 @@
 FAR = 10000.0
 MESH = pl.DeviceIdType.MESH
 UNROLL = 4
-REACH = 4
 VMEM_LIMIT = 8 * 1024 * 1024
 
 SIDES = [(dx, dy) for dx in (-1, 0, 1) for dy in (-1, 0, 1) if (dx, dy) != (0, 0)]
+
+
+CORNERS_FIRST = sorted(SIDES, key=lambda side: -abs(side[0]) - abs(side[1]))
 
 
 def place_of(dx, dy):
@@ -124,19 +126,34 @@
     out,
     disp_v, vel_v, for_v, hei_v, nei_v, count_s, plan_s,
     pos, grid_pos, lists, split, terms, speed_v, up, vp, send_u, send_v, got_u, got_v,
-    local_sem, pos_send, pos_recv, list_send, list_recv, u_send, u_recv, v_send, v_recv, ring,
+    local_sem, pos_send, pos_recv, list_send, list_recv, u_send, u_recv, v_send, v_recv, known,
 ):
     a, b = lax.axis_index("gx"), lax.axis_index("gy")
 
     def at(da, db):
-        return lax.rem(a + da + gx, gx), lax.rem(b + db + gy, gy)
+        return a + da, b + db
+
+    def there(da, db):
+        tests = {-1: a > 0, 0: None, 1: a < gx - 1}[da], {-1: b > 0, 0: None, 1: b < gy - 1}[db]
+        tests = [t for t in tests if t is not None]
+        return tests[0] if len(tests) == 1 else tests[0] & tests[1]
 
     barrier = pltpu.get_barrier_semaphore()
-    greeted = [d for d in range(1, gy) if min(d, gy - d) <= REACH]
-    partners = [at(0, d) for d in greeted]
-    partners += [at(da, db) for da in (-1, 1) for db in (-1, 0, 1)]
-    for partner in partners:
-        pl.semaphore_signal(barrier, inc=1, device_id=partner, device_id_type=MESH)
+    def around(d):
+        return a, lax.rem(b + d + gy, gy)
+
+    for dx, dy in CORNERS_FIRST:
+        if dx != 0:
+
+            @pl.when(there(dx, dy))
+            def _():
+                pl.semaphore_signal(barrier, inc=1, device_id=at(dx, dy), device_id_type=MESH)
+
+    pl.semaphore_signal(barrier, inc=1, device_id=around(-1), device_id_type=MESH)
+
+    @pl.when(b < gy - 1)
+    def _():
+        pl.semaphore_signal(barrier, inc=1, device_id=around(1), device_id_type=MESH)
 
     loads = [
         pltpu.make_async_copy(source, target, local_sem.at[number])
@@ -177,11 +194,13 @@
             up[2 * i + j, 6:8, :] = jnp.broadcast_to(occupied[j : j + 1], (2, 128))
             lists[5 + 4 * i + j] = nei_v[:, i, j, :]
 
-    pl.semaphore_wait(barrier, len(partners))
-
-    copies = []
+    wide = (a > 0).astype(jnp.int32) + (a < gx - 1).astype(jnp.int32)
+    high = 1 + (b > 0).astype(jnp.int32) + (b < gy - 1).astype(jnp.int32)
+    pl.semaphore_wait(barrier, wide * high + 1 + (b > 0).astype(jnp.int32))
+
+    copies = {side: [] for side in SIDES}
     for number, (dx, dy) in enumerate(SIDES):
-        copies.append(
+        copies[dx, dy].append(
             pltpu.make_async_remote_copy(
                 src_ref=pos.at[4],
                 dst_ref=pos.at[place_of(-dx, -dy)],
@@ -193,7 +212,7 @@
         )
     for number, (dx, dy, i, j) in enumerate(LISTS):
         x, y = 1 + i - 2 * dx, 1 + j - 2 * dy
-        copies.append(
+        copies[dx, dy].append(
             pltpu.make_async_remote_copy(
                 src_ref=lists.at[5 + 4 * i + j],
                 dst_ref=lists.at[4 * x + y],
@@ -203,8 +222,47 @@
                 device_id_type=MESH,
             )
         )
-    for copy in copies:
-        copy.start()
+    for dx, dy in CORNERS_FIRST:
+
+        @pl.when(there(dx, dy))
+        def _():
+            for copy in copies[dx, dy]:
+                copy.start()
+
+        @pl.when(jnp.logical_not(there(dx, dy)))
+        def _():
+            for i in near(-dx):
+                for j in near(-dy):
+                    lists[4 * (1 + i + 2 * dx) + 1 + j + 2 * dy] = jnp.zeros((8, 128), jnp.int32)
+
+    half = min(2 * gy // 3, gy - 2)
+
+    def tell(number, target):
+        pl.semaphore_signal(known.at[number], inc=1, device_id=(a, target), device_id_type=MESH)
+
+    @pl.when(b >= 3)
+    def _():
+        pl.semaphore_wait(known.at[0], 1)
+
+    @pl.when((b >= 2) & (b < gy - 1))
+    def _():
+        tell(0, b + 1)
+
+    @pl.when(b == gy - 1)
+    def _():
+        for o in range(gy - 1):
+            tell(2, o)
+
+    @pl.when((b >= 2) & (b <= half))
+    def _():
+        pl.semaphore_wait(known.at[1], 1)
+
+    @pl.when((b >= 1) & (b < half))
+    def _():
+        tell(1, b + 1)
+
+    waits_for_last = (b > half) & (b < gy - 1)
+
     owners = [plan_s[0, 0, 0, c] for c in range(4)]
     place = []
     for c in range(4):
@@ -225,38 +283,49 @@
 
         return of
 
-    of_u = dealt(8, [up[c] for c in range(4)])
-    for d in range(1, gy):
-        send_u[d] = of_u(lax.rem(b + d, gy))
-    got_u[b] = of_u(b)
-
-    u_copies = {}
-    for d in range(1, gy):
-        u_copies[d] = pltpu.make_async_remote_copy(
-            src_ref=send_u.at[d],
-            dst_ref=got_u.at[b],
-            send_sem=u_send.at[d],
-            recv_sem=u_recv.at[d],
-            device_id=at(0, d),
+    def exchange(send, got, send_sem, recv_sem, d):
+        return pltpu.make_async_remote_copy(
+            src_ref=send.at[d],
+            dst_ref=got.at[b],
+            send_sem=send_sem,
+            recv_sem=recv_sem,
+            device_id=around(d),
             device_id_type=MESH,
         )
-    for copy in copies:
-        copy.wait_recv()
-    known = [d for d in range(1, gy) if min(d, gy - d) <= REACH + 1]
-    for d in known:
-        u_copies[d].start()
-    for d in (1, gy - 1):
-        pl.semaphore_signal(ring, inc=1, device_id=at(0, d), device_id_type=MESH)
+
+    def all_of(send, got, send_sem, recv_sem):
+        return pltpu.make_async_remote_copy(
+            src_ref=send.at[pl.ds(0, gy - 1)],
+            dst_ref=got.at[pl.ds(0, gy - 1)],
+            send_sem=send_sem,
+            recv_sem=recv_sem,
+            device_id=around(1),
+            device_id_type=MESH,
+        )
+
+    u_exchange, v_exchange = (send_u, got_u, u_send, u_recv), (send_v, got_v, v_send, v_recv)
+    far_first = sorted(range(1, gy), key=lambda d: -min(d, gy - d))
+
+    of_u = dealt(8, [up[c] for c in range(4)])
+    for d in far_first:
+        send_u[d] = of_u(around(d)[1])
+    got_u[b] = of_u(b)
+    for dx, dy in SIDES:
+
+        @pl.when(there(-dx, -dy))
+        def _():
+            for copy in copies[dx, dy]:
+                copy.wait_recv()
 
     for dx in (-1, 0, 1):
         for dy in (-1, 0, 1):
-            gone = ((a + dx) < 0) | ((a + dx) >= gx) | ((b + dy) < 0) | ((b + dy) >= gy)
-            lift = jnp.where(gone, FAR, 0.0)
             for axis in range(3):
                 for i in range(2):
                     first = axis * 36 + (2 * dx + 2 + i) * 6 + 2 * dy + 2
                     rows = pos[place_of(dx, dy), axis, 2 * i : 2 * i + 2, :]
-                    grid_pos[first : first + 2, :] = rows + lift if axis == 2 else rows
+                    if (dx, dy) != (0, 0):
+                        rows = jnp.where(there(dx, dy), rows, FAR)
+                    grid_pos[first : first + 2, :] = rows
 
     rows16 = [
         (lax.broadcasted_iota(jnp.int32, (16, 128), 0) + 16 * k).astype(jnp.float32).astype(jnp.bfloat16)
@@ -314,11 +383,13 @@
             total = column(step * UNROLL + part, part, total)
         return total
 
+    for d in far_first:
+
+        @pl.when((b + d >= (gy if d > 1 else 0)) & jnp.logical_not(waits_for_last))
+        def _():
+            exchange(*u_exchange, d).start()
+
     total = lax.fori_loop(0, 16 // UNROLL, some_columns, jnp.zeros((24, 128), jnp.float32))
-    pl.semaphore_wait(ring, 2)
-    for d in range(1, gy):
-        if d not in known:
-            u_copies[d].start()
     on_neighbours = total[0:12] + total[12:24]
 
     for t in range(4):
@@ -329,32 +400,54 @@
             speed = speed_v[t, axis : axis + 1, :] + half_step * (force * force_scale)
             vp[t, 2 * axis : 2 * axis + 2, :] = jnp.broadcast_to(speed, (2, 128))
     of_v = dealt(6, [vp[c] for c in range(4)])
-    v_copies = []
-    for d in sorted(range(1, gy), key=lambda d: -min(d, gy - d)):
-        send_v[d] = of_v(lax.rem(b + d, gy))
-        copy = pltpu.make_async_remote_copy(
-            src_ref=send_v.at[d],
-            dst_ref=got_v.at[b],
-            send_sem=v_send.at[d],
-            recv_sem=v_recv.at[d],
-            device_id=at(0, d),
-            device_id_type=MESH,
-        )
-        copy.start()
-        v_copies.append(copy)
+
+    @pl.when(waits_for_last)
+    def _():
+        pl.semaphore_wait(known.at[2], 1)
+
+    for d in far_first:
+        send_v[d] = of_v(around(d)[1])
+
+        @pl.when(b + d >= (gy if d > 1 else 0))
+        def _():
+            exchange(*v_exchange, d).start()
+
     got_v[b] = of_v(b)
-    for copy in u_copies.values():
-        copy.wait_recv()
+
+    @pl.when(b <= half)
+    def _():
+        pl.semaphore_wait(known.at[2], 1)
+
+    for d in range(1, gy):
+
+        @pl.when((b + d >= (gy if d > 1 else 0)) & waits_for_last)
+        def _():
+            exchange(*u_exchange, d).start()
+
+    for d in range(2, gy):
+
+        @pl.when(b + d < gy)
+        def _():
+            exchange(*u_exchange, d).start()
+            exchange(*v_exchange, d).start()
+
+    all_of(*u_exchange).wait_recv()
     for o in range(gy):
         for r in range(4):
             out[0, 0, o, (0, 1, 2, 6)[r], :, :] = got_u[o, 2 * r : 2 * r + 2, :]
-    for copy in v_copies:
-        copy.wait_recv()
+    for dx, dy in SIDES:
+
+        @pl.when(there(dx, dy))
+        def _():
+            for copy in copies[dx, dy]:
+                copy.wait_send()
+
+    all_of(*u_exchange).wait_send()
+    all_of(*v_exchange).wait_recv()
     for o in range(gy):
         for r in range(3):
             out[0, 0, o, r + 3, :, :] = got_v[o, 2 * r : 2 * r + 2, :]
-    for copy in copies + list(u_copies.values()) + v_copies:
-        copy.wait_send()
+    all_of(*v_exchange).wait_send()
 
 
 def per_device(gx, gy, displacement, velocity, forces, heights, counts, neighbours, plan):
@@ -393,11 +486,11 @@
             dma((len(SIDES),)),
             dma((len(LISTS),)),
             dma((len(LISTS),)),
-            dma((gy,)),
-            dma((gy,)),
-            dma((gy,)),
-            dma((gy,)),
-            pltpu.SemaphoreType.REGULAR,
+            dma,
+            dma,
+            dma,
+            dma,
+            pltpu.SemaphoreType.REGULAR((3,)),
         ],
         compiler_params=pltpu.CompilerParams(
             collective_id=0, has_side_effects=True, vmem_limit_bytes=VMEM_LIMIT

time: 31.2 us -> 29.1 us (0.933)
  the two profiles are of different devices: /device:TPU:1 before, /device:TPU:32 now
where the time goes in v3:
time: 29.1 us; the launch traced here: 29 us
  Pallas kernels  28.3 us (97%)
  local copies, waits for them, and re-layouts  0.64 us (2%)
    pallas_call x1, Pallas kernels, per_device(): pl.pallas_call(functools.partial(kernel, gx, gy), out_shape=jax.ShapeDtyp...  28.3 us
    unnamed x1, local copies, waits for them, and re-layouts  0.64 us

profile of v3, /device:TPU:32, one launch (start us, length us, event | category | flops | bytes accessed | tf_op | source)
XLA Modules:
  0.0 29.0 jit_solution(12655792794544115755)
XLA Ops:
  0.0 28.3 %verlet_recut.1 = f32[1,1,12,7,2,128]{5,4,3,2,1,0:T(2,128)S(1)} custom-call(f32[3,2,2,128]{3,2,1,0:T(2,128)} %displacement.1, f32[3,2,2,128]{3,2,1,0:T(2,128)} %velocity.1, f32[3,2,2,128]{3,2,1,0:T(2,128)} %forces.1, s32[2,2,128]{2,1,0:T(2,128)} %heights.1, s32[2,2]{1,0:T(2,128)} %counts.1, s32[8,2,2,128]{3,2,1,0:T(2,128)} %neighbours.1, s32[1,1,1,4]{3,2,1,0:T(1,128)} %bitcast.3), custom_call_target="tpu_custom_call" | custom-call | tf_op jit(solution)/shard_map/verlet_recut/pallas_call | solution.py:459
  28.3 0.6 %copy.9 = f32[1,1,12,2,7,128]{5,3,4,2,1,0:T(2,128)} copy(f32[1,1,12,2,7,128]{5,3,4,2,1,0:T(2,128)S(1)} %bitcast.2) | data formatting | bytes 172032

commit v4 on v3

--- a/solution.py
+++ b/solution.py
@@ -38,9 +38,6 @@
 
 def near(d):
     return {-1: (0,), 0: (0, 1), 1: (1,)}[d]
-
-
-LISTS = [(dx, dy, i, j) for dx, dy in SIDES for i in near(dx) for j in near(dy)]
 
 
 def poly_sin(x):
@@ -192,7 +189,7 @@
                 up[2 * i + j, 2 * axis : 2 * axis + 2, :] = jnp.broadcast_to(offset[j : j + 1], (2, 128))
         for j in range(2):
             up[2 * i + j, 6:8, :] = jnp.broadcast_to(occupied[j : j + 1], (2, 128))
-            lists[5 + 4 * i + j] = nei_v[:, i, j, :]
+            lists[1 + i, 1 + j] = nei_v[:, i, j, :]
 
     wide = (a > 0).astype(jnp.int32) + (a < gx - 1).astype(jnp.int32)
     high = 1 + (b > 0).astype(jnp.int32) + (b < gy - 1).astype(jnp.int32)
@@ -210,12 +207,13 @@
                 device_id_type=MESH,
             )
         )
-    for number, (dx, dy, i, j) in enumerate(LISTS):
-        x, y = 1 + i - 2 * dx, 1 + j - 2 * dy
+    for number, (dx, dy) in enumerate(SIDES):
+        here = tuple(pl.ds(1 + near(d)[0], len(near(d))) for d in (dx, dy))
+        over = tuple(pl.ds(1 + near(d)[0] - 2 * d, len(near(d))) for d in (dx, dy))
         copies[dx, dy].append(
             pltpu.make_async_remote_copy(
-                src_ref=lists.at[5 + 4 * i + j],
-                dst_ref=lists.at[4 * x + y],
+                src_ref=lists.at[here],
+                dst_ref=lists.at[over],
                 send_sem=list_send.at[number],
                 recv_sem=list_recv.at[number],
                 device_id=at(dx, dy),
@@ -233,7 +231,7 @@
         def _():
             for i in near(-dx):
                 for j in near(-dy):
-                    lists[4 * (1 + i + 2 * dx) + 1 + j + 2 * dy] = jnp.zeros((8, 128), jnp.int32)
+                    lists[1 + i + 2 * dx, 1 + j + 2 * dy] = jnp.zeros((8, 128), jnp.int32)
 
     half = min(2 * gy // 3, gy - 2)
 
@@ -333,10 +331,10 @@
     ]
     one, none = jnp.ones((16, 128), jnp.bfloat16), jnp.zeros((16, 128), jnp.bfloat16)
 
-    def column(k, part, total):
+    def gradients(k):
         x, y = 1 + k // 4, 1 + k % 4
         base = (x - 1) * 6 + y - 1
-        entries = lists[k]
+        entries = lists[k // 4, k % 4]
         slot, offset = entries & 127, entries >> 7
         near_by = [None] * 3
         for c in range(9):
@@ -351,6 +349,11 @@
         grads = column_terms(center, near_by)
         for axis in range(3):
             terms[k, axis] = grads[axis]
+
+    def scattered(k, part, grads, total):
+        x, y = 1 + k // 4, 1 + k % 4
+        entries = lists[k // 4, k % 4]
+        slot, offset = entries & 127, entries >> 7
         highs = [g.astype(jnp.bfloat16).astype(jnp.float32) for g in grads]
         lows = [g - h for g, h in zip(grads, highs)]
         for t in range(4):
@@ -379,8 +382,11 @@
         return total
 
     def some_columns(step, total):
+        before = [step * UNROLL - UNROLL + part for part in range(UNROLL)]
+        grads = [[terms[k, axis] for axis in range(3)] for k in before]
         for part in range(UNROLL):
-            total = column(step * UNROLL + part, part, total)
+            total = scattered(before[part], part, grads[part], total)
+            gradients(step * UNROLL + part)
         return total
 
     for d in far_first:
@@ -389,7 +395,12 @@
         def _():
             exchange(*u_exchange, d).start()
 
-    total = lax.fori_loop(0, 16 // UNROLL, some_columns, jnp.zeros((24, 128), jnp.float32))
+    for part in range(UNROLL):
+        gradients(part)
+    total = lax.fori_loop(1, 16 // UNROLL, some_columns, jnp.zeros((24, 128), jnp.float32))
+    for part in range(UNROLL):
+        k = 16 - UNROLL + part
+        total = scattered(k, part, [terms[k, axis] for axis in range(3)], total)
     on_neighbours = total[0:12] + total[12:24]
 
     for t in range(4):
@@ -471,7 +482,7 @@
             pltpu.SMEM((1, 1, 1, 4), jnp.int32),
             pltpu.VMEM((9, 3, 4, 128), f32),
             pltpu.VMEM((112, 128), f32),
-            pltpu.VMEM((16, 8, 128), jnp.int32),
+            pltpu.VMEM((4, 4, 8, 128), jnp.int32),
             pltpu.VMEM((UNROLL * 192, 128), f32),
             pltpu.VMEM((16, 3, 8, 128), f32),
             pltpu.VMEM((4, 8, 128), f32),
@@ -484,8 +495,8 @@
             dma((7,)),
             dma((len(SIDES),)),
             dma((len(SIDES),)),
-            dma((len(LISTS),)),
-            dma((len(LISTS),)),
+            dma((len(SIDES),)),
+            dma((len(SIDES),)),
             dma,
             dma,
             dma,

time: 29.1 us -> 28.5 us (0.979)
  Pallas kernels: 28.3 us -> 27.6 us
    pallas_call x1, Pallas kernels: 28.3 us -> 27.6 us  [per_device(): pl.pallas_call(functools.partial(kernel, gx, gy), out_shape=jax.ShapeDtyp...]
where the time goes in v4:
time: 28.5 us; the launch traced here: 28.3 us
  Pallas kernels  27.6 us (97%)
  local copies, waits for them, and re-layouts  0.64 us (2%)
    pallas_call x1, Pallas kernels, per_device(): pl.pallas_call(functools.partial(kernel, gx, gy), out_shape=jax.ShapeDtyp...  27.6 us
    unnamed x1, local copies, waits for them, and re-layouts  0.64 us

profile of v4, /device:TPU:32, one launch (start us, length us, event | category | flops | bytes accessed | tf_op | source)
XLA Modules:
  0.0 28.3 jit_solution(2697969604296045131)
XLA Ops:
  0.0 27.6 %verlet_recut.1 = f32[1,1,12,7,2,128]{5,4,3,2,1,0:T(2,128)S(1)} custom-call(f32[3,2,2,128]{3,2,1,0:T(2,128)} %displacement.1, f32[3,2,2,128]{3,2,1,0:T(2,128)} %velocity.1, f32[3,2,2,128]{3,2,1,0:T(2,128)} %forces.1, s32[2,2,128]{2,1,0:T(2,128)} %heights.1, s32[2,2]{1,0:T(2,128)} %counts.1, s32[8,2,2,128]{3,2,1,0:T(2,128)} %neighbours.1, s32[1,1,1,4]{3,2,1,0:T(1,128)} %bitcast.3), custom_call_target="tpu_custom_call" | custom-call | tf_op jit(solution)/shard_map/verlet_recut/pallas_call | solution.py:470
  27.6 0.6 %copy.9 = f32[1,1,12,2,7,128]{5,3,4,2,1,0:T(2,128)} copy(f32[1,1,12,2,7,128]{5,3,4,2,1,0:T(2,128)S(1)} %bitcast.2) | data formatting | bytes 172032

commit v5 on v4

--- a/solution.py
+++ b/solution.py
@@ -23,7 +23,7 @@
 
 FAR = 10000.0
 MESH = pl.DeviceIdType.MESH
-UNROLL = 4
+UNROLL = 8
 VMEM_LIMIT = 8 * 1024 * 1024
 
 SIDES = [(dx, dy) for dx in (-1, 0, 1) for dy in (-1, 0, 1) if (dx, dy) != (0, 0)]
@@ -397,7 +397,7 @@
 
     for part in range(UNROLL):
         gradients(part)
-    total = lax.fori_loop(1, 16 // UNROLL, some_columns, jnp.zeros((24, 128), jnp.float32))
+    total = some_columns(1, jnp.zeros((24, 128), jnp.float32))
     for part in range(UNROLL):
         k = 16 - UNROLL + part
         total = scattered(k, part, [terms[k, axis] for axis in range(3)], total)

time: 28.5 us -> 28.3 us (level)
  no operation moved by 1% of the time
where the time goes in v5:
time: 28.3 us; the launch traced here: 28.1 us
  Pallas kernels  27.4 us (97%)
  local copies, waits for them, and re-layouts  0.64 us (2%)
    pallas_call x1, Pallas kernels, per_device(): pl.pallas_call(functools.partial(kernel, gx, gy), out_shape=jax.ShapeDtyp...  27.4 us
    unnamed x1, local copies, waits for them, and re-layouts  0.64 us

profile of v5, /device:TPU:32, one launch (start us, length us, event | category | flops | bytes accessed | tf_op | source)
XLA Modules:
  0.0 28.1 jit_solution(9710944114208913303)
XLA Ops:
  0.0 27.4 %verlet_recut.1 = f32[1,1,12,7,2,128]{5,4,3,2,1,0:T(2,128)S(1)} custom-call(f32[3,2,2,128]{3,2,1,0:T(2,128)} %displacement.1, f32[3,2,2,128]{3,2,1,0:T(2,128)} %velocity.1, f32[3,2,2,128]{3,2,1,0:T(2,128)} %forces.1, s32[2,2,128]{2,1,0:T(2,128)} %heights.1, s32[2,2]{1,0:T(2,128)} %counts.1, s32[8,2,2,128]{3,2,1,0:T(2,128)} %neighbours.1, s32[1,1,1,4]{3,2,1,0:T(1,128)} %bitcast.3), custom_call_target="tpu_custom_call" | custom-call | tf_op jit(solution)/shard_map/verlet_recut/pallas_call | solution.py:470
  27.4 0.6 %copy.9 = f32[1,1,12,2,7,128]{5,3,4,2,1,0:T(2,128)} copy(f32[1,1,12,2,7,128]{5,3,4,2,1,0:T(2,128)S(1)} %bitcast.2) | data formatting | bytes 172032
